TPU v7x, 32 devices: a whole 2x2x4 slice. The times are simulated.
32 devices in a mesh: row: 4 (over z), col: 8 (over y, x, core).
Axes of the slice: x: 2, y: 2, z: 4, core: 2. Of those that a mesh axis runs over, the one named last changes fastest.
Arguments:
- matrix: float32 [8192, 8192], P('row', 'col'), may hold values from -2.5 to 2.5
Outputs:
- squared: float32 [8192, 8192], P('row', 'col')
- frob: float32 [], replicated
All inputs are finite; a program needn't handle non-finite values.
Results may differ from a plain program's by a relative error of at most 0.0001.
Values sent between devices are 32-bit elements; how exact they have to be, the bound alone decides.
A program may use at most 64 MiB of HBM per device.

v0:
```python
import jax
import jax.numpy as jnp
from jax import lax
from jax.sharding import PartitionSpec as P

KP = 256


def broadcast(value, axis, source):
    kept = jnp.where(lax.axis_index(axis) == source, value, 0).astype(value.dtype)
    return lax.psum(kept, axis)


def offsets(matrix, step):
    row_block = matrix.shape[0]
    col_block = matrix.shape[1]
    total = row_block * lax.axis_size("row")
    start = step * (total // 4)
    return (start // col_block, start % col_block, start // row_block, start % row_block)


def fetch_rows(matrix, step):
    col_owner, local_col, row_owner, local_row = offsets(matrix, step)
    return broadcast(matrix[local_row : local_row + KP, :], "row", row_owner)


def product(left, right):
    return jnp.dot(left, right, preferred_element_type=jnp.float32, precision=lax.Precision.HIGHEST)


def body(matrix):
    column_index = lax.axis_index("col")
    slots = []
    for step in range(4):
        col_owner, local_col, row_owner, local_row = offsets(matrix, step)
        panel = matrix[:, local_col : local_col + KP]
        slots.append(jnp.where(column_index == col_owner, panel, jnp.zeros_like(panel)))
    stacked = lax.psum(jnp.concatenate(slots, axis=1), "col")
    rights = jnp.concatenate([fetch_rows(matrix, step) for step in range(4)], axis=0)
    squared = product(stacked, rights)
    total = lax.psum(jnp.sum(squared * squared), ("row", "col"))
    order_size = matrix.shape[0] * lax.axis_size("row")
    frob = jnp.sqrt(total) / order_size
    return (squared, frob)


def solution(mesh):
    placed = (P("row", "col"),)
    return jax.shard_map(
        body, mesh=mesh, in_specs=placed, out_specs=(P("row", "col"), P()), check_vma=False
    )
```

profile of v0, /device:TPU:0, one launch (start us, length us, event | category | flops | bytes accessed | tf_op | source)
XLA Modules:
  0.0 378.5 jit_solution(3300064162137872236)
XLA Ops:
  7.2 0.0 all-reduce.6.cloned.1.call-start
  7.2 3.4 slice_select_fusion.7
  10.7 0.0 all-reduce.6.cloned.1.call-update
  10.7 0.0 all-reduce.4.cloned.1.call-start
  10.7 2.2 slice_select_fusion.3
  13.0 4.1 %pad_maximum_fusion = f32[2048,1024]{1,0:T(8,128)} fusion(f32[2048,256]{1,0:T(8,128)S(1)} %get-tuple-element.13, f32[2048,256]{1,0:T(8,128)S(1)} %get-tuple-element.12, f32[2048,256]{1,0:T(8,128)S(1)} %get-tuple-element.11, f32[2048,256]{1,0:T(8,128)S(1)} %get-tuple-element.10), kind=kLoop, calls=%fused_computation | loop fusion | flops 6291456 | bytes 16777216 | tf_op jit(solution)/shard_map/concatenate | solution.py:38
  17.0 0.0 all-reduce.4.cloned.1.call-update
  17.1 151.5 %all-reduce.6.cloned.1.call-done = (f32[256,1024]{1,0:T(8,128)}, f32[256,1024]{1,0:T(8,128)}, f32[256,1024]{1,0:T(8,128)}, f32[256,1024]{1,0:T(8,128)}) async-done(((f32[256,1024]{1,0:T(8,128)}, f32[256,1024]{1,0:T(8,128)}, f32[256,1024]{1,0:T(8,128)}, f32[256,1024]{1,0:T(8,128)}), (f32[256,1024]{1,0:T(8,128)}, f32[256,1024]{1,0:T(8,128)}, f32[256,1024]{1,0:T(8,128)}, ...) | async-done | bytes 4194320 | tf_op jit(solution)/shard_map/psum | solution.py:11
  168.6 129.3 %all-reduce.4.cloned.1.call-done = f32[2048,1024]{1,0:T(8,128)} async-done(((f32[2048,1024]{1,0:T(8,128)}), f32[2048,1024]{1,0:T(8,128)}) %all-reduce.4.cloned.1.call-update) | async-done | bytes 8388624 | tf_op jit(solution)/shard_map/psum | solution.py:38
  297.8 32.3 %multiply_reduce_fusion = (f32[]{:T(128)}, f32[2048,1024]{1,0:T(8,128)}) fusion(f32[2048,1024]{1,0:T(8,128)} %all-reduce.4.cloned.1.call-done, f32[256,1024]{1,0:T(8,128)} %get-tuple-element.2, f32[256,1024]{1,0:T(8,128)} %get-tuple-element.3, f32[256,1024]{1,0:T(8,128)} %get-tuple-element.4, f32[256,1024]{1,0:T(8,128)} %get-tuple-element.5), kind=kOutput, calls=%fused_computation.1 | convolution fusion | flops 25777143808 | bytes 20971524 | tf_op jit(solution)/shard_map/dot_general | solution.py:28
  330.2 39.6 %psum.47 = f32[]{:T(128)} all-reduce(f32[]{:T(128)} %get-tuple-element.14), channel_id=1, replica_groups=mesh['row'=4,'col'=8] {'row','col'}, use_global_device_ids=true, to_apply=%region_6.7 | all-reduce | flops 1 | bytes 8 | tf_op jit(solution)/shard_map/psum | solution.py:41
Async XLA Ops:
  7.2 161.4 %all-reduce.6.cloned.1.call-start = ((), (), s32[]{:S(2)}) async-start(), calls=%async_computation.1 | async-start | bytes 8388608 | tf_op jit(solution)/shard_map/psum | solution.py:11
  10.7 287.2 %all-reduce.4.cloned.1.call-start = ((), (), s32[]{:S(2)}) async-start(), calls=%async_computation | async-start | bytes 16777216 | tf_op jit(solution)/shard_map/psum | solution.py:38
Sparse Core Ops, SparseCore 0:
  10.8 157.7 all-reduce.5
  172.6 125.1 all-reduce.3
where the time goes:
time: 379 us; the launch traced here: 378 us
  waiting for transfers between devices  281 us (74%)
  blocking collectives  39.6 us (10%)
  matrix products  32.3 us (9%)
  between operations  15.9 us (4%)
  other arithmetic  9.73 us (3%)
    psum x1, waiting for transfers between devices, broadcast(): return lax.psum(kept, axis)  152 us
    psum x1, waiting for transfers between devices, body(): stacked = lax.psum(jnp.concatenate(slots, axis=1), 'col')  129 us
    psum x1, blocking collectives, body(): total = lax.psum(jnp.sum(squared * squared), ('row', 'col'))  39.6 us
    dot_general x1, matrix products, product(): jnp.dot(left, right, preferred_element_type=jnp.float32, precision=lax.Pr...  32.3 us
  transfers between devices with their start and end apart: 2, of which 2 were waited for; matrix products, arithmetic and copies ran while one was open for 2% of the time, Pallas kernels for 0%

commit v1 on v0

--- a/solution.py
+++ b/solution.py
@@ -8,7 +8,7 @@
 
 def broadcast(value, axis, source):
     kept = jnp.where(lax.axis_index(axis) == source, value, 0).astype(value.dtype)
-    return lax.psum(kept, axis)
+    return jnp.sum(lax.all_gather(kept, axis), 0)
 
 
 def offsets(matrix, step):

time: 379 us -> 421 us (1.11)
  waiting for transfers between devices: 281 us -> 311 us
  other arithmetic: 9.73 us -> 21.7 us
    all_gather x0 -> x4, waiting for transfers between devices: none -> 309 us  [broadcast(): return jnp.sum(lax.all_gather(kept, axis), 0)]
    psum x1 -> x0, waiting for transfers between devices: 152 us -> none  [broadcast(): return lax.psum(kept, axis)]
    psum x1, waiting for transfers between devices: 129 us -> 0.01 us  [body(): stacked = lax.psum(jnp.concatenate(slots, axis=1), 'col')]
    reduce_sum x0 -> x4, other arithmetic: none -> 11.9 us  [broadcast(): return jnp.sum(lax.all_gather(kept, axis), 0)]
  transfers between devices with their start and end apart: 2 -> 5, of which waited for: 2 -> 4; matrix products, arithmetic and copies ran while one was open for 2% -> 4% of each run, Pallas kernels for 0% -> 0%
where the time goes in v1:
time: 421 us
  waiting for transfers between devices  311 us (74%)
  blocking collectives  38.9 us (9%)
  matrix products  31.7 us (8%)
  other arithmetic  21.7 us (5%)
  between operations  17.1 us (4%)
    all_gather x4, waiting for transfers between devices, broadcast(): return jnp.sum(lax.all_gather(kept, axis), 0)  309 us
    psum x1, blocking collectives, body(): total = lax.psum(jnp.sum(squared * squared), ('row', 'col'))  38.9 us
    dot_general x1, matrix products, product(): jnp.dot(left, right, preferred_element_type=jnp.float32, precision=lax.Pr...  31.7 us
    reduce_sum x4, other arithmetic, broadcast(): return jnp.sum(lax.all_gather(kept, axis), 0)  11.9 us
  transfers between devices with their start and end apart: 5, of which 4 were waited for; matrix products, arithmetic and copies ran while one was open for 4% of the time, Pallas kernels for 0%

profile of v1, /device:TPU:0, one launch (start us, length us, event | category | flops | bytes accessed | tf_op | source)
XLA Modules:
  0.0 420.9 jit_solution(2547100847027480211)
XLA Ops:
  8.0 0.0 all-gather.9.cloned.1.call-start
  8.1 3.5 slice_select_fusion.7
  11.6 0.0 all-gather.9.cloned.1.call-update
  11.6 0.0 all-gather.11.cloned.1.call-start
  11.6 0.7 all-gather.11.cloned.1.call-update
  12.3 0.0 all-gather.13.cloned.1.call-start
  12.4 0.7 all-gather.13.cloned.1.call-update
  13.1 0.0 all-gather.15.cloned.1.call-start
  13.1 0.5 all-gather.15.cloned.1.call-update
  13.7 0.0 all-reduce.2.cloned.1.call-start
  13.7 2.2 slice_select_fusion.3
  16.0 4.1 pad_maximum_fusion
  20.0 0.0 all-reduce.2.cloned.1.call-update
  20.0 75.2 %all-gather.9.cloned.1.call-done = f32[1024,1024]{1,0:T(8,128)} async-done(((f32[256,1024]{1,0:T(8,128)}), f32[1024,1024]{1,0:T(8,128)}) %all-gather.9.cloned.1.call-update) | async-done | bytes 4194320 | tf_op jit(solution)/shard_map/all_gather | solution.py:11
  95.2 2.7 reduce_sum.45
  97.9 78.1 %all-gather.11.cloned.1.call-done = f32[1024,1024]{1,0:T(8,128)} async-done(((f32[256,1024]{1,0:T(8,128)}), f32[1024,1024]{1,0:T(8,128)}) %all-gather.11.cloned.1.call-update) | async-done | bytes 4194320 | tf_op jit(solution)/shard_map/all_gather | solution.py:11
  176.0 2.7 reduce_sum.46
  178.8 78.1 %all-gather.13.cloned.1.call-done = f32[1024,1024]{1,0:T(8,128)} async-done(((f32[256,1024]{1,0:T(8,128)}), f32[1024,1024]{1,0:T(8,128)}) %all-gather.13.cloned.1.call-update) | async-done | bytes 4194320 | tf_op jit(solution)/shard_map/all_gather | solution.py:11
  256.9 2.7 reduce_sum.47
  259.6 78.0 %all-gather.15.cloned.1.call-done = f32[1024,1024]{1,0:T(8,128)} async-done(((f32[256,1024]{1,0:T(8,128)}), f32[1024,1024]{1,0:T(8,128)}) %all-gather.15.cloned.1.call-update) | async-done | bytes 4194320 | tf_op jit(solution)/shard_map/all_gather | solution.py:11
  337.5 3.8 reduce_sum.48
  341.3 0.0 all-reduce.2.cloned.1.call-done
  341.3 31.7 %multiply_reduce_fusion = (f32[]{:T(128)}, f32[2048,1024]{1,0:T(8,128)}) fusion(f32[2048,1024]{1,0:T(8,128)} %all-reduce.2.cloned.1.call-done, f32[256,1024]{1,0:T(8,128)} %reduce_sum.48, f32[256,1024]{1,0:T(8,128)S(1)} %reduce_sum.47, f32[256,1024]{1,0:T(8,128)S(1)} %reduce_sum.46, f32[256,1024]{1,0:T(8,128)S(1)} %reduce_sum.45), kind=kOutput, calls=%fused_computation.1 | convolution fusion | flops 25777143808 | bytes 20971524 | tf_op jit(solution)/shard_map/dot_general | solution.py:28
  373.0 38.9 %psum.15 = f32[]{:T(128)} all-reduce(f32[]{:T(128)} %get-tuple-element.10), channel_id=1, replica_groups=mesh['row'=4,'col'=8] {'row','col'}, use_global_device_ids=true, to_apply=%region_6.7 | all-reduce | flops 1 | bytes 8 | tf_op jit(solution)/shard_map/psum | solution.py:41
Async XLA Ops:
  8.0 87.2 %all-gather.9.cloned.1.call-start = ((), (), s32[]{:S(2)}) async-start(), calls=%async_computation.1 | async-start | bytes 5242880 | tf_op jit(solution)/shard_map/all_gather | solution.py:11
  11.6 164.4 %all-gather.11.cloned.1.call-start = ((), (), s32[]{:S(2)}) async-start(), calls=%async_computation.2 | async-start | bytes 5242880 | tf_op jit(solution)/shard_map/all_gather | solution.py:11
  12.3 244.5 %all-gather.13.cloned.1.call-start = ((), (), s32[]{:S(2)}) async-start(), calls=%async_computation.3 | async-start | bytes 5242880 | tf_op jit(solution)/shard_map/all_gather | solution.py:11
  13.1 324.5 %all-gather.15.cloned.1.call-start = ((), (), s32[]{:S(2)}) async-start(), calls=%async_computation.4 | async-start | bytes 5242880 | tf_op jit(solution)/shard_map/all_gather | solution.py:11
  13.7 327.7 %all-reduce.2.cloned.1.call-start = ((), (), s32[]{:S(2)}) async-start(), calls=%async_computation | async-start | bytes 16777216 | tf_op jit(solution)/shard_map/psum | solution.py:38
Sparse Core Ops, SparseCore 0:
  11.7 83.4 all-gather.8
  96.8 79.2 all-gather.10
  177.6 79.2 all-gather.12
  258.3 79.2 all-gather.14
Sparse Core Ops, SparseCore 1:
  20.1 128.6 all-reduce.1
